TPU v7x, 256 devices: a whole 4x4x8 slice. The times are simulated.
256 devices in a mesh: field: 32 (over z, x), vrow: 2 (over core), vcol: 4 (over y).
Axes of the slice: x: 4, y: 4, z: 8, core: 2. Of those that a mesh axis runs over, the one named last changes fastest.
Arguments:
- blocks: bfloat16 [1024, 192, 2, 256], P(('vrow', 'vcol'), 'field'), may hold values from 0 to 1
- block_ids: int32 [8, 32, 6], P(('vrow', 'vcol'), 'field'), may hold values from 0 to 11, as said below
- block_counts: int32 [8, 32], P(('vrow', 'vcol'), 'field'), may hold values from 1 to 6, as said below
Outputs:
- tables: float32 [1024, 2, 2, 4, 2, 128], P(('vrow', 'field'), None, None, 'vcol')
Inputs may be any that keep to these rules, and one draw needn't show every extreme that they name: `block_ids`: within each row of the last dimension the entries are distinct. `block_counts`: 6 is reached in every draw.
All inputs are finite; a program needn't handle non-finite values.
Results may differ from a plain program's by a relative error of at most 0.0003.
Values may be sent and summed in bfloat16 or wider, within the bound.
No kernel may reach another device: no remote copies, remote signals or barrier semaphores. Data moves between devices by JAX's collectives and lax.ppermute only.
A program may use at most 64 MiB of HBM per device.

v0:
```python
import math
import jax
import jax.numpy as jnp
from jax import lax
from jax.sharding import PartitionSpec as P

SBLK = 12
BLOCK = 256


def side_by_side(arrays, axis, dim, along):
    widths = [math.prod(a.shape[along:]) for a in arrays]
    both = jnp.concatenate(
        [a.reshape(*a.shape[:along], w) for a, w in zip(arrays, widths)], axis=along
    )
    out = lax.all_gather(both, axis, axis=dim, tiled=True)
    parts = jnp.split(out, [sum(widths[:k]) for k in range(1, len(widths))], axis=along)
    return tuple((b.reshape(*out.shape[:along], *a.shape[along:]) for a, b in zip(arrays, parts)))


def split_up(array, dim, length):
    dims = array.shape
    parts = array.reshape(*dims[:dim], length, dims[dim] // length, *dims[dim + 1 :])
    return jnp.moveaxis(parts, dim, 0)


def sent_and_summed(array, axis, dim):
    length = lax.axis_size(axis)
    parts = lax.all_to_all(split_up(array, dim, length), axis, 0, 0, tiled=True)
    return jnp.sum(parts, axis=0)


def expand(blocks, block_ids, block_counts):
    shards = block_ids.shape[0]
    occ = block_ids.shape[-1]
    shaped = blocks.reshape(shards, blocks.shape[0] // shards, occ, 2, blocks.shape[-1])
    slots = jnp.arange(occ, dtype=jnp.int32)
    live = slots[None, :] < block_counts[:, 0][:, None]
    onehot = (block_ids[:, 0, :, None] == jnp.arange(SBLK, dtype=jnp.int32)[None, None, :]) & live[
        ..., None
    ]
    dense = jnp.einsum(
        "sok,svocx->svkcx", onehot.astype(jnp.bfloat16), shaped, preferred_element_type=jnp.float32
    )
    return dense.astype(jnp.bfloat16).reshape(blocks.shape[0], SBLK, 2, blocks.shape[-1])


def on_device(blocks, block_ids, block_counts):
    row_data, row_ids, row_counts = (
        lax.all_gather(blocks, "vcol", axis=0, tiled=True),
        *side_by_side((block_ids, block_counts), "vcol", 0, 2),
    )
    rows = expand(row_data, row_ids, row_counts)
    col_data, col_ids, col_counts = (
        lax.all_gather(blocks, "vrow", axis=0, tiled=True),
        *side_by_side((block_ids, block_counts), "vrow", 0, 2),
    )
    columns = expand(col_data, col_ids, col_counts)
    groups = lax.axis_size("vrow")
    columns = columns.reshape(groups, columns.shape[0] // groups, SBLK, 2, columns.shape[-1])
    fields = lax.axis_size("field")
    term = jnp.einsum("ikcx,rjkdx->icrdj", rows, columns, preferred_element_type=jnp.float32)
    summed = sent_and_summed(term[:, :, :, None], "field", 0)
    return summed / (fields * SBLK * BLOCK)


def solution(mesh):
    placed = (
        P(("vrow", "vcol"), "field", None, None),
        P(("vrow", "vcol"), "field", None),
        P(("vrow", "vcol"), "field"),
    )
    return jax.shard_map(
        on_device,
        mesh=mesh,
        in_specs=placed,
        out_specs=P(("vrow", "field"), None, None, "vcol", None, None),
        check_vma=False,
    )
```

profile of v0, /device:TPU:2, one launch (start us, length us, event | category | flops | bytes accessed | tf_op | source)
XLA Modules:
  0.0 164.3 jit_solution(4973293619530026705)
XLA Ops:
  6.5 0.0 all-gather.3.cloned.1.call-start
  6.5 0.7 all-gather.3.cloned.1.call-update
  7.3 0.0 all-gather.5.cloned.1.call-start
  7.3 0.7 all-gather.5.cloned.1.call-update
  8.7 0.7 pad_add_fusion
  9.4 1.8 %all_gather.12 = s32[2,1,7]{2,1,0:T(1,128)S(1)} all-gather(s32[1,1,7]{2,1,0:T(1,128)S(1)} %pad_add_fusion), channel_id=1, replica_groups=mesh['field'=32,'vrow'=2,'vcol'=4] {'vrow'}, dimensions={0}, use_global_device_ids=true | all-gather | bytes 84 | tf_op jit(solution)/shard_map/all_gather | solution.py:16
  11.2 10.0 %all_gather.14 = s32[4,1,7]{2,1,0:T(1,128)S(1)} all-gather(s32[1,1,7]{2,1,0:T(1,128)S(1)} %pad_add_fusion), channel_id=1, replica_groups=mesh['field'=32,'vrow'=2,'vcol'=4] {'vcol'}, dimensions={0}, use_global_device_ids=true | all-gather | bytes 140 | tf_op jit(solution)/shard_map/all_gather | solution.py:16
  21.1 0.2 slice_reduce_fusion.1
  21.3 0.2 slice_reduce_fusion
  21.6 0.1 iota_compare_fusion.2
  21.6 0.1 iota_compare_fusion.3
  21.7 5.5 %all-gather.3.cloned.1.call-done = bf16[256,6,2,256]{3,2,1,0:T(2,128)(2,1)} async-done(((bf16[128,6,2,256]{3,2,1,0:T(2,128)(2,1)}), bf16[256,6,2,256]{3,2,1,0:T(2,128)(2,1)}) %all-gather.3.cloned.1.call-update) | async-done | bytes 1572880 | tf_op jit(solution)/shard_map/all_gather | solution.py:55
  27.2 1.9 %copy.9 = bf16[256,6,2,256]{3,1,2,0:T(8,128)(2,1)S(1)} copy(bf16[256,6,2,256]{3,2,1,0:T(2,128)(2,1)} %all-gather.3.cloned.1.call-done) | data formatting | bytes 3145728 | tf_op jit(solution)/shard_map/all_gather | solution.py:55
  29.1 3.1 %convert_bitcast_fusion = bf16[2,128,12,2,256,1]{4,2,3,1,0,5:T(8,128)(2,1)} fusion(bf16[2,128,6,2,256]{4,2,3,1,0:T(8,128)(2,1)S(1)} %bitcast.39, s32[2,6]{1,0:T(2,128)S(1)} %bitcast.42, pred[2,6]{1,0:T(4,128)(4,1)S(1)} %iota_compare_fusion.3), kind=kOutput, calls=%fused_computation.3 | convolution fusion | flops 20447520 | bytes 4718652 | tf_op jit(solution)/shard_map/sok,svocx->svkcx/dot_general | solution.py:42
  32.2 40.3 %all-gather.5.cloned.1.call-done = bf16[512,6,2,256]{3,2,1,0:T(2,128)(2,1)} async-done(((bf16[128,6,2,256]{3,2,1,0:T(2,128)(2,1)}), bf16[512,6,2,256]{3,2,1,0:T(2,128)(2,1)}) %all-gather.5.cloned.1.call-update) | async-done | bytes 3145744 | tf_op jit(solution)/shard_map/all_gather | solution.py:50
  72.4 2.9 %copy.10 = bf16[512,6,2,256]{3,1,2,0:T(8,128)(2,1)S(1)} copy(bf16[512,6,2,256]{3,2,1,0:T(2,128)(2,1)} %all-gather.5.cloned.1.call-done) | data formatting | bytes 6291456 | tf_op jit(solution)/shard_map/all_gather | solution.py:50
  75.3 0.0 copy-start
  75.3 4.4 %convolution_convert_fusion = bf16[4,12,128,2,256]{4,1,3,2,0:T(8,128)(2,1)S(1)} fusion(bf16[4,128,6,2,256]{4,2,3,1,0:T(8,128)(2,1)S(1)} %bitcast.37, s32[4,6]{1,0:T(4,128)S(1)} %bitcast.41, pred[4,6]{1,0:T(4,128)(4,1)S(1)} %iota_compare_fusion.2), kind=kOutput, calls=%fused_computation | convolution fusion | flops 40895040 | bytes 9437304 | tf_op jit(solution)/shard_map/sok,svocx->svkcx/dot_general | solution.py:42
  79.8 0.0 copy-done
  79.8 14.4 %fusion.3 = f32[512,2,2,2,128]{0,4,1,3,2:T(8,128)} fusion(bf16[512,12,2,256,1,1]{3,1,2,0,5,4:T(8,128)(2,1)S(1)} %bitcast.38, bf16[2,128,12,2,256,1]{4,2,3,1,0,5:T(8,128)(2,1)S(1)} %copy-done), kind=kOutput, calls=%fused_computation.5 | convolution fusion | flops 3221225472 | bytes 11534336 | tf_op jit(solution)/shard_map/ikcx,rjkdx->icrdj/dot_general | solution.py:62
  94.2 1.9 %copy.13 = f32[512,2,2,2,128]{4,0,3,2,1:T(8,128)S(1)} copy(f32[512,2,2,2,128]{0,4,1,3,2:T(8,128)} %fusion.3) | data formatting | bytes 4194304 | tf_op jit(solution)/shard_map/ikcx,rjkdx->icrdj/transpose | solution.py:62
  96.1 0.3 copy.14
  96.3 60.3 %all_to_all.5 = f32[32,16,2,2,1,2,128]{6,1,5,3,2,4,0:T(8,128)S(1)} all-to-all(f32[32,16,2,2,1,2,128]{6,1,5,3,2,4,0:T(8,128)S(1)} %copy.14), channel_id=1, replica_groups=mesh['field'=32,'vrow'=2,'vcol'=4] {'field'}, dimensions={0} | all-to-all | bytes 4194304 | tf_op jit(solution)/shard_map/all_to_all | solution.py:29
  156.6 0.1 reduce_sum.9
  156.8 0.7 copy.16
  (1 shorter events, 0.0 us)
Async XLA Ops:
  6.5 20.7 %all-gather.3.cloned.1.call-start = ((), (), s32[]{:S(2)}) async-start(), calls=%async_computation.1 | async-start | bytes 2359296 | tf_op jit(solution)/shard_map/all_gather | solution.py:55
  7.3 65.2 %all-gather.5.cloned.1.call-start = ((), (), s32[]{:S(2)}) async-start(), calls=%async_computation.2 | async-start | bytes 3932160 | tf_op jit(solution)/shard_map/all_gather | solution.py:50
  75.3 4.5 %copy-start = (bf16[2,128,12,2,256,1]{4,2,3,1,0,5:T(8,128)(2,1)S(1)}, bf16[2,128,12,2,256,1]{4,2,3,1,0,5:T(8,128)(2,1)}, u32[]{:S(2)}) copy-start(bf16[2,128,12,2,256,1]{4,2,3,1,0,5:T(8,128)(2,1)} %convert_bitcast_fusion) | copy-start | bytes 9437188
Sparse Core Ops, SparseCore 0:
  9.1 18.0 all-gather.2
  29.1 43.3 all-gather.4
where the time goes:
time: 165 us; the launch traced here: 164 us
  blocking collectives  72.1 us (44%)
  waiting for transfers between devices  47.2 us (29%)
  matrix products  21.9 us (13%)
  between operations  14.1 us (9%)
  local copies, waits for them, and re-layouts  7.99 us (5%)
    all_to_all x1, blocking collectives, sent_and_summed(): parts = lax.all_to_all(split_up(array, dim, length), axis, 0, 0, tiled=True)  60.3 us
    all_gather x1, waiting for transfers between devices, on_device(): lax.all_gather(blocks, 'vcol', axis=0, tiled=True)  40.3 us
    dot_general x1, matrix products, on_device(): jnp.einsum('ikcx,rjkdx->icrdj', rows, columns, preferred_element_type=jnp...  14.4 us
    all_gather x2, blocking collectives, side_by_side(): out = lax.all_gather(both, axis, axis=dim, tiled=True)  11.8 us
    dot_general x2, matrix products, expand(): jnp.einsum('sok,svocx->svkcx', onehot.astype(jnp.bfloat16), shaped, prefe...  7.51 us
    all_gather x1, waiting for transfers between devices, on_device(): lax.all_gather(blocks, 'vrow', axis=0, tiled=True)  5.53 us
  transfers between devices with their start and end apart: 2, of which 2 were waited for; matrix products, arithmetic and copies ran while one was open for 4% of the time, Pallas kernels for 0%

commit v1 on v0

--- a/solution.py
+++ b/solution.py
@@ -46,8 +46,34 @@
 
 
 def on_device(blocks, block_ids, block_counts):
+
+    def press_words(body):
+        link_axis = "vcol"
+        later = lax.axis_size(link_axis)
+        v1 = lax.axis_index(link_axis)
+        state_next, f_next, local_out = (later, v1, body.shape[0])
+        in_order = [(dev, (dev + 1) % state_next) for dev in range(state_next)]
+        inbox = [(dev, (dev - 1) % state_next) for dev in range(state_next)]
+        after = jnp.zeros((*body.shape[:0], state_next * local_out, *body.shape[1:]), body.dtype)
+        piece_next = n_now = body
+        after = lax.dynamic_update_slice_in_dim(after, body, f_next * local_out, axis=0)
+        arr_next = state_next // 2
+        i = 1
+        while i < arr_next + 1:
+            piece_next = lax.ppermute(piece_next, link_axis, perm=in_order)
+            after = lax.dynamic_update_slice_in_dim(
+                after, piece_next, (f_next - i) % state_next * local_out, axis=0
+            )
+            if i < state_next - arr_next:
+                n_now = lax.ppermute(n_now, link_axis, perm=inbox)
+                after = lax.dynamic_update_slice_in_dim(
+                    after, n_now, (f_next + i) % state_next * local_out, axis=0
+                )
+            i += 1
+        return after
+
     row_data, row_ids, row_counts = (
-        lax.all_gather(blocks, "vcol", axis=0, tiled=True),
+        press_words(blocks),
         *side_by_side((block_ids, block_counts), "vcol", 0, 2),
     )
     rows = expand(row_data, row_ids, row_counts)

time: 165 us -> 151 us (0.915)
  waiting for transfers between devices: 47.2 us -> 15.8 us
  blocking collectives: 72.1 us -> 79.8 us
  local copies, waits for them, and re-layouts: 7.99 us -> 12.3 us
  starting transfers between devices: 0.04 us -> 3.26 us
  matrix products: 21.9 us -> 24.2 us
    all_gather x1 -> x0, waiting for transfers between devices: 40.3 us -> none  [on_device(): lax.all_gather(blocks, 'vcol', axis=0, tiled=True)]
    ppermute x0 -> x3, waiting for transfers between devices: none -> 15.8 us  [the longest x2 15.8 us: press_words(): piece_next = lax.ppermute(piece_next, link_axis, perm=in_order)]
    all_gather x2, blocking collectives: 11.8 us -> 20.7 us  [side_by_side(): out = lax.all_gather(both, axis, axis=dim, tiled=True)]
    all_gather x1, waiting for transfers between devices: 5.53 us -> 0.01 us  [on_device(): lax.all_gather(blocks, 'vrow', axis=0, tiled=True)]
    dynamic_update_slice x0 -> x4, local copies, waits for them, and re-layouts: none -> 4.82 us  [the longest x2 2.36 us: press_words(): lax.dynamic_update_slice_in_dim(after, piece_next, (f_next - i) % state_n...]
    ppermute x0 -> x3, starting transfers between devices: none -> 3.25 us  [the longest x1 1.66 us: press_words(): n_now = lax.ppermute(n_now, link_axis, perm=inbox)]
    all_gather x1 -> x0, local copies, waits for them, and re-layouts: 2.87 us -> none  [on_device(): lax.all_gather(blocks, 'vcol', axis=0, tiled=True)]
    dot_general x2, matrix products: 7.51 us -> 9.82 us  [expand(): jnp.einsum('sok,svocx->svkcx', onehot.astype(jnp.bfloat16), shaped, prefe...]
  transfers between devices with their start and end apart: 2 -> 4, of which waited for: 2 -> 1; matrix products, arithmetic and copies ran while one was open for 4% -> 11% of each run, Pallas kernels for 0% -> 0%
where the time goes in v1:
time: 151 us
  blocking collectives  79.8 us (53%)
  matrix products  24.2 us (16%)
  waiting for transfers between devices  15.8 us (10%)
  between operations  14.2 us (9%)
  local copies, waits for them, and re-layouts  12.3 us (8%)
  starting transfers between devices  3.26 us (2%)
    all_to_all x1, blocking collectives, sent_and_summed(): parts = lax.all_to_all(split_up(array, dim, length), axis, 0, 0, tiled=True)  59.1 us
    all_gather x2, blocking collectives, side_by_side(): out = lax.all_gather(both, axis, axis=dim, tiled=True)  20.7 us
    ppermute x2, waiting for transfers between devices, press_words(): piece_next = lax.ppermute(piece_next, link_axis, perm=in_order)  15.8 us
    dot_general x1, matrix products, on_device(): jnp.einsum('ikcx,rjkdx->icrdj', rows, columns, preferred_element_type=jnp...  14.4 us
    dot_general x2, matrix products, expand(): jnp.einsum('sok,svocx->svkcx', onehot.astype(jnp.bfloat16), shaped, prefe...  9.82 us
  transfers between devices with their start and end apart: 4, of which 1 were waited for; matrix products, arithmetic and copies ran while one was open for 11% of the time, Pallas kernels for 0%

profile of v1, /device:TPU:2, one launch (start us, length us, event | category | flops | bytes accessed | tf_op | source)
XLA Modules:
  0.0 150.6 jit_solution(2258951376881681822)
XLA Ops:
  6.5 0.0 copy-start.1
  6.5 0.0 all-gather.2.cloned.1.call-start
  6.5 1.6 %collective-permute-start = (bf16[128,6,2,256]{3,2,1,0:T(2,128)(2,1)}, bf16[128,6,2,256]{3,2,1,0:T(2,128)(2,1)S(1)}, u32[]{:S(2)}, u32[]{:S(2)}) collective-permute-start(bf16[128,6,2,256]{3,2,1,0:T(2,128)(2,1)} %param.3), channel_id=1, source_target_pairs={{0,1},{1,2},{2,3},{3,0},{4,5},{5,6},{6,7},{7,4},{8,9},{9,10},{10,1... | collective-permute-start | bytes 2359304 | tf_op jit(solution)/shard_map/ppermute | solution.py:63
  8.1 1.7 %collective-permute-start.1 = (bf16[128,6,2,256]{3,2,1,0:T(2,128)(2,1)}, bf16[128,6,2,256]{3,2,1,0:T(2,128)(2,1)S(1)}, u32[]{:S(2)}, u32[]{:S(2)}) collective-permute-start(bf16[128,6,2,256]{3,2,1,0:T(2,128)(2,1)} %param.3), channel_id=1, source_target_pairs={{0,3},{1,0},{2,1},{3,2},{4,7},{5,4},{6,5},{7,6},{8,11},{9,8},{10,9... | collective-permute-start | bytes 2359304 | tf_op jit(solution)/shard_map/ppermute | solution.py:68
  10.4 0.7 pad_add_fusion
  11.2 0.0 all-gather.2.cloned.1.call-update
  11.2 1.8 %all_gather.9 = s32[2,1,7]{2,1,0:T(1,128)S(1)} all-gather(s32[1,1,7]{2,1,0:T(1,128)S(1)} %pad_add_fusion), channel_id=1, replica_groups=mesh['field'=32,'vrow'=2,'vcol'=4] {'vrow'}, dimensions={0}, use_global_device_ids=true | all-gather | bytes 84 | tf_op jit(solution)/shard_map/all_gather | solution.py:16
  13.0 18.9 %all_gather.11 = s32[4,1,7]{2,1,0:T(1,128)S(1)} all-gather(s32[1,1,7]{2,1,0:T(1,128)S(1)} %pad_add_fusion), channel_id=1, replica_groups=mesh['field'=32,'vrow'=2,'vcol'=4] {'vcol'}, dimensions={0}, use_global_device_ids=true | all-gather | bytes 140 | tf_op jit(solution)/shard_map/all_gather | solution.py:16
  31.9 0.2 slice_reduce_fusion
  32.1 2.3 %broadcast_in_dim.2 = bf16[512,6,2,256]{3,1,2,0:T(8,128)(2,1)} broadcast(bf16[]{:T(256)} %constant.32.clone.1), dimensions={} | broadcast | bytes 3145730 | tf_op jit(solution)/shard_map/broadcast_in_dim | solution.py:57
  34.4 0.0 copy-done.1
  34.4 1.3 copy_dynamic-update-slice_fusion.3
  35.7 0.1 iota_compare_fusion.2
  35.7 0.0 collective-permute-done
  35.7 0.0 collective-permute-start.2
  35.8 0.2 slice_reduce_fusion.1
  36.0 0.1 iota_compare_fusion.3
  36.1 1.2 copy_dynamic-update-slice_fusion.2
  37.3 0.0 collective-permute-done.1
  37.3 1.2 copy_dynamic-update-slice_fusion.1
  38.5 15.8 %collective-permute-done.2 = bf16[128,6,2,256]{3,2,1,0:T(2,128)(2,1)S(1)} collective-permute-done((bf16[128,6,2,256]{3,2,1,0:T(2,128)(2,1)S(1)}, bf16[128,6,2,256]{3,2,1,0:T(2,128)(2,1)S(1)}, u32[]{:S(2)}, u32[]{:S(2)}) %collective-permute-start.2) | collective-permute-done | bytes 786464 | tf_op jit(solution)/shard_map/ppermute | solution.py:63
  54.2 1.2 copy_dynamic-update-slice_fusion
  55.4 7.9 %convolution_convert_fusion = bf16[4,128,2,256,12]{3,4,2,1,0:T(8,128)(2,1)} fusion(bf16[4,128,6,2,256]{4,2,3,1,0:T(8,128)(2,1)} %bitcast.7, s32[4,6]{1,0:T(4,128)S(1)} %bitcast.40, pred[4,6]{1,0:T(4,128)(4,1)S(1)} %iota_compare_fusion.2), kind=kOutput, calls=%fused_computation | convolution fusion | flops 40895040 | bytes 9437304 | tf_op jit(solution)/shard_map/sok,svocx->svkcx/dot_general | solution.py:42
  63.3 2.0 %copy.15 = bf16[256,6,2,256]{3,1,2,0:T(8,128)(2,1)S(1)} copy(bf16[256,6,2,256]{3,2,1,0:T(2,128)(2,1)} %all-gather.2.cloned.1.call-done) | data formatting | bytes 3145728 | tf_op jit(solution)/shard_map/all_gather | solution.py:81
  65.3 2.0 %convert_bitcast_fusion = bf16[2,128,12,2,256,1]{4,2,3,1,0,5:T(8,128)(2,1)S(1)} fusion(bf16[2,128,6,2,256]{4,2,3,1,0:T(8,128)(2,1)S(1)} %bitcast.38, s32[2,6]{1,0:T(2,128)S(1)} %bitcast.41, pred[2,6]{1,0:T(4,128)(4,1)S(1)} %iota_compare_fusion.3), kind=kOutput, calls=%fused_computation.3 | convolution fusion | flops 20447520 | bytes 4718652 | tf_op jit(solution)/shard_map/sok,svocx->svkcx/dot_general | solution.py:42
  67.2 0.0 copy-done
  67.3 14.4 %fusion.3 = f32[512,2,2,2,128]{0,4,1,3,2:T(8,128)} fusion(bf16[512,12,2,256,1,1]{3,1,2,0,5,4:T(8,128)(2,1)S(1)} %bitcast.37, bf16[2,128,12,2,256,1]{4,2,3,1,0,5:T(8,128)(2,1)S(1)} %convert_bitcast_fusion), kind=kOutput, calls=%fused_computation.5 | convolution fusion | flops 3221225472 | bytes 11534336 | tf_op jit(solution)/shard_map/ikcx,rjkdx->icrdj/dot_general | solution.py:88
  81.6 1.9 %copy.22 = f32[512,2,2,2,128]{4,0,3,2,1:T(8,128)S(1)} copy(f32[512,2,2,2,128]{0,4,1,3,2:T(8,128)} %fusion.3) | data formatting | bytes 4194304 | tf_op jit(solution)/shard_map/ikcx,rjkdx->icrdj/transpose | solution.py:88
  83.6 0.3 copy.23
  83.8 59.1 %all_to_all.5 = f32[32,16,2,2,1,2,128]{6,1,5,3,2,4,0:T(8,128)S(1)} all-to-all(f32[32,16,2,2,1,2,128]{6,1,5,3,2,4,0:T(8,128)S(1)} %copy.23), channel_id=1, replica_groups=mesh['field'=32,'vrow'=2,'vcol'=4] {'field'}, dimensions={0} | all-to-all | bytes 4194304 | tf_op jit(solution)/shard_map/all_to_all | solution.py:29
  142.9 0.1 reduce_sum.9
  143.0 0.7 copy.25
  (3 shorter events, 0.0 us)
Async XLA Ops:
  6.5 27.9 %copy-start.1 = (bf16[128,6,2,256]{3,2,1,0:T(2,128)(2,1)S(1)}, bf16[128,6,2,256]{3,2,1,0:T(2,128)(2,1)}, u32[]{:S(2)}) copy-start(bf16[128,6,2,256]{3,2,1,0:T(2,128)(2,1)} %param.3) | copy-start | bytes 2359300
  6.5 56.7 %all-gather.2.cloned.1.call-start = ((), (), s32[]{:S(2)}) async-start(), calls=%async_computation.1 | async-start | bytes 2359296 | tf_op jit(solution)/shard_map/all_gather | solution.py:81
  6.5 29.2 %collective-permute-start = (bf16[128,6,2,256]{3,2,1,0:T(2,128)(2,1)}, bf16[128,6,2,256]{3,2,1,0:T(2,128)(2,1)S(1)}, u32[]{:S(2)}, u32[]{:S(2)}) collective-permute-start(bf16[128,6,2,256]{3,2,1,0:T(2,128)(2,1)} %param.3), channel_id=1, source_target_pairs={{0,1},{1,2},{2,3},{3,0},{4,5},{5,6},{6,7},{7,4},{8,9},{9,10},{10,1... | collective-permute-start | bytes 2359304 | tf_op jit(solution)/shard_map/ppermute | solution.py:63
  8.1 29.2 %collective-permute-start.1 = (bf16[128,6,2,256]{3,2,1,0:T(2,128)(2,1)}, bf16[128,6,2,256]{3,2,1,0:T(2,128)(2,1)S(1)}, u32[]{:S(2)}, u32[]{:S(2)}) collective-permute-start(bf16[128,6,2,256]{3,2,1,0:T(2,128)(2,1)} %param.3), channel_id=1, source_target_pairs={{0,3},{1,0},{2,1},{3,2},{4,7},{5,4},{6,5},{7,6},{8,11},{9,8},{10,9... | collective-permute-start | bytes 2359304 | tf_op jit(solution)/shard_map/ppermute | solution.py:68
  35.7 18.5 %collective-permute-start.2 = (bf16[128,6,2,256]{3,2,1,0:T(2,128)(2,1)S(1)}, bf16[128,6,2,256]{3,2,1,0:T(2,128)(2,1)S(1)}, u32[]{:S(2)}, u32[]{:S(2)}) collective-permute-start(bf16[128,6,2,256]{3,2,1,0:T(2,128)(2,1)S(1)} %collective-permute-done), channel_id=1, source_target_pairs={{0,1},{1,2},{2,3},{3,0},{4,5},{5,6},{6,7},{7,4},{8,9},{9,10},{10,1... | collective-permute-start | bytes 2359304 | tf_op jit(solution)/shard_map/ppermute | solution.py:63
  63.3 4.0 %copy-start = (bf16[4,128,2,256,12]{3,4,2,1,0:T(8,128)(2,1)S(1)}, bf16[4,128,2,256,12]{3,4,2,1,0:T(8,128)(2,1)}, u32[]{:S(2)}) copy-start(bf16[4,128,2,256,12]{3,4,2,1,0:T(8,128)(2,1)} %convolution_convert_fusion) | copy-start | bytes 18874372
Sparse Core Ops, SparseCore 0:
  11.3 16.8 all-gather.1
